TPU v7x, 256 devices: a whole 4x4x8 slice. The times are simulated.
256 devices in a mesh: ctx: 32 (over x, y, core), tp: 8 (over z).
Axes of the slice: x: 4, y: 4, z: 8, core: 2. Of those that a mesh axis runs over, the one named last changes fastest.
Arguments:
- patches: bfloat16 [16384, 1280], P('ctx'), may hold values from -21 to 21
- window_ids: int32 [16384], P('ctx'), may hold values from -1 to 4095, as said below
- positions: int32 [4096], P('ctx'), may hold values from 0 to 32768, as said below
- text_embed: bfloat16 [32768, 8192], P('ctx', 'tp'), may hold values from -6 to 6
- cotangent: bfloat16 [32768, 8192], P('ctx', 'tp'), may hold values from -0.119628906 to 0.119628906
- qkv_weight: bfloat16 [3, 1280, 1280], P(None, None, 'tp'), may hold values from -0.15625 to 0.15625
- out_weight: bfloat16 [1280, 1280], P('tp'), may hold values from -0.15625 to 0.15625
- merger_weight: bfloat16 [5120, 8192], P('ctx', 'tp'), may hold values from -0.078125 to 0.078125
- norm_gain: bfloat16 [8192], P('tp'), may hold values from 0.099609375 to 1.8984375
Outputs:
- normed: bfloat16 [32768, 8192], P('ctx', 'tp')
- merger_grad: float32 [5120, 8192], P('ctx', 'tp')
Inputs may be any that keep to these rules, and one draw needn't show every extreme that they name: `window_ids`: windows are runs of consecutive patch slots of one index of ctx, each of 4 to 64 slots and a multiple of 4; every window id belongs to one index of ctx; the padding slots of an index of ctx come after its live slots and carry -1. Merged slot j of an index of ctx covers its patch slots 4j to 4j+3 and is live exactly when those are; live slots carry distinct positions, dead ones carry 32768. The live slots of one index of ctx name at most 4 positions among the 1024 positions of any one index of ctx.
All inputs are finite; a program needn't handle non-finite values.
Results may differ from a plain program's by a relative error of at most 0.014.
Values may be sent and summed in bfloat16 or wider, within the bound.
A program may use at most 128 MiB of HBM per device.

v0:
```python
import jax
import jax.numpy as jnp
from jax import lax
from jax.sharding import PartitionSpec as P

D = 8192
HEAD_DIM = 80


def sent_to_all(shard, axis):
    copies = jnp.broadcast_to(shard, (lax.axis_size(axis), *shard.shape))
    return lax.all_to_all(copies, axis, split_axis=0, concat_axis=0, tiled=True)


def taken_together(shard, axis):
    return sent_to_all(shard, axis).sum(axis=0)


def in_one(arrays, axis):
    ends = [0]
    for a in arrays:
        ends.append(ends[-1] + a.size)
    so_far = taken_together(jnp.concatenate([a.ravel() for a in arrays]), axis)
    return tuple((so_far[b:e].reshape(a.shape) for a, b, e in zip(arrays, ends, ends[1:])))


def window_attention(patches, window_ids, qkv_weight):
    slot_rows = patches.shape[0]
    projected = [
        jnp.dot(patches, qkv_weight[i], preferred_element_type=jnp.float32).astype(jnp.bfloat16)
        for i in range(3)
    ]
    local_heads = qkv_weight.shape[2] // HEAD_DIM
    queries = projected[0].reshape(slot_rows, local_heads, HEAD_DIM)
    keys_all = projected[1].reshape(slot_rows, local_heads, HEAD_DIM)
    values = projected[2].reshape(slot_rows, local_heads, HEAD_DIM)
    width = min(512, slot_rows)
    factor = 1.0 / HEAD_DIM**0.5

    def one_block(block_index):
        scores = (
            jnp.einsum("qhd,khd->hqk", queries, keys_all, preferred_element_type=jnp.float32)
            * factor
        )
        allowed = (window_ids[:, None] == window_ids[None, :]) & (window_ids[None, :] >= 0)
        scores = jnp.where(allowed[None], scores, jnp.float32(-1e30))
        highest = jnp.max(scores, axis=2, keepdims=True)
        weights = jnp.exp(scores - highest)
        probs = (weights / jnp.sum(weights, axis=2, keepdims=True)).astype(jnp.bfloat16)
        attended = jnp.einsum("hqk,khd->qhd", probs, values, preferred_element_type=jnp.float32)
        return attended.astype(jnp.bfloat16).reshape(width, local_heads * HEAD_DIM)

    blocks = lax.map(one_block, jnp.arange(slot_rows // width, dtype=jnp.int32))
    return blocks.reshape(slot_rows, local_heads * HEAD_DIM)


def contract_rows(left, right):
    return lax.dot_general(
        left, right, (((0,), (0,)), ((), ())), preferred_element_type=jnp.float32
    )


def shards(
    patches,
    window_ids,
    positions,
    text_embed,
    cotangent,
    qkv_weight,
    out_weight,
    merger_weight,
    norm_gain,
):
    ctx_size = lax.axis_size("ctx")
    slots = positions.shape[0]
    tok_rows = text_embed.shape[0]
    bucket_size = slots // ctx_size
    attended = window_attention(patches, window_ids, qkv_weight)
    partial_out = jnp.dot(attended, out_weight, preferred_element_type=jnp.float32)
    summed = lax.psum(partial_out.astype(jnp.bfloat16), "tp").astype(jnp.float32)
    hidden = (patches.astype(jnp.float32) + summed).astype(jnp.bfloat16)
    merged_in = hidden.reshape(slots, 4 * hidden.shape[1])
    columns = lax.all_to_all(merged_in, "ctx", split_axis=1, concat_axis=0, tiled=True)
    chosen = merged_in
    merged = jnp.dot(
        chosen,
        lax.all_gather(merger_weight, "ctx", axis=0, tiled=True),
        preferred_element_type=jnp.float32,
    ).astype(jnp.bfloat16)
    target = positions // tok_rows
    hits = (target[:, None] == jnp.arange(ctx_size, dtype=jnp.int32)[None, :]).astype(jnp.int32)
    ranks = jnp.sum(jnp.cumsum(hits, axis=0) * hits, axis=1) - 1
    bucket = jnp.where(target < ctx_size, target * bucket_size + ranks, -1)
    select = jnp.arange(slots, dtype=jnp.int32)[:, None] == bucket[None, :]
    select_mat = select.astype(jnp.bfloat16)
    outgoing = jnp.dot(select_mat, merged, preferred_element_type=jnp.float32).astype(jnp.bfloat16)
    local_row = positions % tok_rows
    occupied = jnp.any(select, axis=1)
    out_rows = jnp.where(occupied, jnp.sum(jnp.where(select, local_row[None, :], 0), axis=1), -1)
    incoming, in_rows = (
        lax.all_to_all(outgoing, "ctx", split_axis=0, concat_axis=0, tiled=True),
        lax.all_to_all(out_rows, "ctx", split_axis=0, concat_axis=0, tiled=True),
    )
    placed = jnp.arange(tok_rows, dtype=jnp.int32)[:, None] == in_rows[None, :]
    placed_mat = placed.astype(jnp.bfloat16)
    vision = jnp.dot(placed_mat, incoming, preferred_element_type=jnp.float32)
    is_vision = jnp.any(placed, axis=1)
    embedded = jnp.where(is_vision[:, None], vision, text_embed.astype(jnp.float32))
    gain_vec = norm_gain.astype(jnp.float32)[None, :]
    gained = gain_vec * cotangent.astype(jnp.float32)
    squares, inner = in_one(
        (jnp.sum(embedded * embedded, axis=1), jnp.sum(embedded * gained, axis=1)), "tp"
    )
    scale = lax.rsqrt(squares / D + 1e-06)[:, None]
    normed = (embedded * scale * gain_vec).astype(jnp.bfloat16)
    d_embed = (scale * gained - embedded * scale**3 * inner[:, None] / D).astype(jnp.bfloat16)
    back_rows = contract_rows(placed_mat, d_embed).astype(jnp.bfloat16)
    returned = lax.all_to_all(back_rows, "ctx", split_axis=0, concat_axis=0, tiled=True)
    d_merged = contract_rows(select_mat, returned).astype(jnp.bfloat16)
    chosen = columns
    merger_grad = contract_rows(chosen, lax.all_gather(d_merged, "ctx", axis=0, tiled=True))
    return (normed, merger_grad)


def solution(mesh):
    in_specs = (
        P("ctx", None),
        P("ctx"),
        P("ctx"),
        P("ctx", "tp"),
        P("ctx", "tp"),
        P(None, None, "tp"),
        P("tp", None),
        P("ctx", "tp"),
        P("tp"),
    )
    out_specs = (P("ctx", "tp"), P("ctx", "tp"))
    return jax.shard_map(shards, mesh=mesh, in_specs=in_specs, out_specs=out_specs, check_vma=False)
```

profile of v0, /device:TPU:1, one launch (start us, length us, event | category | flops | bytes accessed | tf_op | source)
XLA Modules:
  0.0 239.2 jit_solution(6177392035362610401)
XLA Ops:
  8.1 2.1 convolution_convert_fusion.7
  10.2 2.0 convolution_convert_fusion.5
  12.2 1.6 convolution_convert_fusion.6
  15.0 1.2 convolution_convert_fusion.4
  16.3 1.6 convolution_convert_fusion
  19.9 8.6 %all-to-all-start = ((s32[32,4,1]{1,2,0:T(1,128)}), s32[32,4,1]{1,2,0:T(1,128)S(1)}, u32[]{:S(2)}, u32[]{:S(2)}) async-start(s32[32,4,1]{1,2,0:T(1,128)} %bitcast), calls=%async_computation | async-start | bytes 32768 | tf_op jit(solution)/shard_map/all_to_all | solution.py:102
  28.5 66.8 %all-reduce.2.cloned.1.call-done = bf16[512,1280]{1,0:T(8,128)(2,1)} async-done(((bf16[512,1280]{1,0:T(8,128)(2,1)}), bf16[512,1280]{1,0:T(8,128)(2,1)}) %all-reduce.2.cloned.1.call-update) | async-done | bytes 1310736 | tf_op jit(solution)/shard_map/psum | solution.py:80
  95.3 1.6 add_convert_fusion
  97.8 5.7 %convolution_convert_fusion.2 = bf16[128,1024]{1,0:T(8,128)(2,1)S(1)} fusion(bf16[128,5120]{1,0:T(8,128)(2,1)S(1)} %reshape.118, bf16[5120,1024]{1,0:T(8,128)(2,1)} %all-gather.3.cloned.1.call-done, s32[128]{0:T(128)S(1)} %compare_select_fusion), kind=kOutput, calls=%fused_computation.19 | convolution fusion | flops 1376010240 | bytes 12059136 | tf_op jit(solution)/shard_map/dot_general | solution.py:96
  104.3 11.4 %all-to-all-start.1 = ((bf16[32,4,1024]{2,1,0:T(4,128)(2,1)}), bf16[32,4,1024]{2,1,0:T(4,128)(2,1)S(1)}, u32[]{:S(2)}, u32[]{:S(2)}) async-start(bf16[32,4,1024]{2,1,0:T(4,128)(2,1)} %all_to_all.39), calls=%async_computation.1 | async-start | bytes 524288 | tf_op jit(solution)/shard_map/all_to_all | solution.py:101
  115.8 3.9 %copy.37 = bf16[1024,1024]{0,1:T(8,128)(2,1)} copy(bf16[1024,1024]{1,0:T(8,128)(2,1)} %param.13) | data formatting | bytes 4194304 | tf_op args[4]
  119.7 4.0 %copy.36 = bf16[1024,1024]{0,1:T(8,128)(2,1)} copy(bf16[1024,1024]{1,0:T(8,128)(2,1)} %param.12) | data formatting | bytes 4194304 | tf_op args[3]
  125.2 5.6 %multiply_reduce_fusion.1 = (f32[1024]{0:T(1024)S(1)}, f32[1024]{0:T(1024)S(1)}, f32[1024,1024]{0,1:T(8,128)}) fusion(bf16[1024,1024]{0,1:T(8,128)(2,1)} %copy.37, f32[1024]{0:T(1024)S(1)} %convert_element_type.78, bf16[1024,1024]{0,1:T(8,128)(2,1)} %copy.36, bf16[128,1024]{1,0:T(8,128)(2,1)S(1)} %all_to_all.41, s32[128]{0:T(128)S(1)} %eq.74, ...), kind=kOutput, calls=%fused_computation.5 | convolution fusion | flops 276953088 | bytes 8664576 | tf_op jit(solution)/shard_map/dot_general | solution.py:106
  130.9 11.2 %all_to_all.55 = f32[8,1,2048]{2,1,0:T(1,128)S(1)} all-to-all(f32[8,1,2048]{2,1,0:T(1,128)S(1)} %broadcast_in_dim.73), channel_id=1, replica_groups=mesh['ctx'=32,'tp'=8] {'tp'}, dimensions={0} | all-to-all | bytes 131072 | tf_op jit(solution)/shard_map/all_to_all | solution.py:12
  142.2 4.3 %fusion.6 = bf16[128,1024]{1,0:T(8,128)(2,1)S(1)} fusion(f32[1024,1024]{0,1:T(8,128)} %get-tuple-element.37, bf16[1024,1024]{0,1:T(8,128)(2,1)} %copy.37, f32[1024]{0:T(1024)S(1)} %get-tuple-element.34, f32[1024]{0:T(1024)S(1)} %get-tuple-element.32, f32[1024]{0:T(1024)S(1)} %get-tuple-element.33, f32[1024]{0:T(1024)S(1)} %convert_element_type.78, ...), kind=kOutput, calls=%fused_computation.17 | convolution fusion | flops 277217280 | bytes 6570496 | tf_op jit(solution)/shard_map/dot_general | solution.py:58
  146.5 17.6 %all_to_all.56 = bf16[32,4,1024]{2,1,0:T(4,128)(2,1)S(1)} all-to-all(bf16[32,4,1024]{2,1,0:T(4,128)(2,1)S(1)} %all_to_all.47), channel_id=1, replica_groups=mesh['ctx'=32,'tp'=8] {'ctx'}, dimensions={0} | all-to-all | bytes 524288 | tf_op jit(solution)/shard_map/all_to_all | solution.py:118
  165.2 3.6 %all_to_all.43 = bf16[128,32,160]{2,1,0:T(8,128)(2,1)} reshape(bf16[512,1280]{1,0:T(8,128)(2,1)S(1)} %add_convert_fusion) | data formatting | bytes 2621440 | tf_op jit(solution)/shard_map/all_to_all | solution.py:83
  168.8 4.4 %copy.39 = bf16[128,32,160]{0,2,1:T(8,128)(2,1)} copy(bf16[128,32,160]{2,1,0:T(8,128)(2,1)} %all_to_all.43) | data formatting | bytes 2621440 | tf_op jit(solution)/shard_map/all_to_all | solution.py:83
  173.2 4.5 %all-to-all-start.3 = ((bf16[128,32,160]{0,2,1:T(8,128)(2,1)}), bf16[128,32,160]{0,2,1:T(8,128)(2,1)}, u32[]{:S(2)}, u32[]{:S(2)}) async-start(bf16[128,32,160]{0,2,1:T(8,128)(2,1)} %copy.39), calls=%async_computation.3 | async-start | bytes 2621440 | tf_op jit(solution)/shard_map/all_to_all | solution.py:83
  177.7 2.6 %multiply_convert_fusion = bf16[1024,1024]{0,1:T(8,128)(2,1)S(1)} fusion(f32[1024,1024]{0,1:T(8,128)} %get-tuple-element.37, f32[1024]{0:T(1024)S(1)} %get-tuple-element.33, f32[1024]{0:T(1024)S(1)} %convert_element_type.78), kind=kLoop, calls=%fused_computation.2 | loop fusion | flops 3145728 | bytes 6299648 | tf_op jit(solution)/shard_map/convert_element_type | solution.py:115
  180.3 2.6 %copy.41 = bf16[1024,1024]{1,0:T(8,128)(2,1)} copy(bf16[1024,1024]{0,1:T(8,128)(2,1)S(1)} %multiply_convert_fusion) | data formatting | bytes 4194304
  182.9 15.3 %all-to-all-done.3 = bf16[128,32,160]{0,2,1:T(8,128)(2,1)} async-done(((bf16[128,32,160]{0,2,1:T(8,128)(2,1)}), bf16[128,32,160]{0,2,1:T(8,128)(2,1)}, u32[]{:S(2)}, u32[]{:S(2)}) %all-to-all-start.3) | async-done | bytes 1310752 | tf_op jit(solution)/shard_map/all_to_all | solution.py:83
  198.2 27.4 %all-gather.5.cloned.1.call-done = bf16[4096,1024]{1,0:T(8,128)(2,1)} async-done(((bf16[128,1024]{1,0:T(8,128)(2,1)}), bf16[4096,1024]{1,0:T(8,128)(2,1)}) %all-gather.5.cloned.1.call-update) | async-done | bytes 8388624 | tf_op jit(solution)/shard_map/all_gather | solution.py:121
  225.6 6.2 %fusion.3 = f32[160,1024]{1,0:T(8,128)} fusion(bf16[4096,1024]{1,0:T(8,128)(2,1)} %all-gather.5.cloned.1.call-done, bf16[128,32,160]{0,2,1:T(8,128)(2,1)} %all-to-all-done.3), kind=kOutput, calls=%fused_computation.14 | convolution fusion | flops 1342177280 | bytes 10354688 | tf_op jit(solution)/shard_map/dot_general | solution.py:58
  (46 shorter events, 7.8 us)
Async XLA Ops:
  8.0 8.3 %copy-start = (bf16[160,1280]{1,0:T(8,128)(2,1)S(1)}, bf16[160,1280]{1,0:T(8,128)(2,1)}, u32[]{:S(2)}) copy-start(bf16[160,1280]{1,0:T(8,128)(2,1)} %param.15) | copy-start | bytes 1228804
  8.0 4.1 %copy-start.1 = (bf16[512,1280]{1,0:T(8,128)(2,1)S(1)}, bf16[512,1280]{1,0:T(8,128)(2,1)}, u32[]{:S(2)}) copy-start(bf16[512,1280]{1,0:T(8,128)(2,1)} %param.9) | copy-start | bytes 3932164
  8.0 87.3 %all-reduce.2.cloned.1.call-start = ((), (), s32[]{:S(2)}) async-start(), calls=%async_computation.5 | async-start | bytes 2621440 | tf_op jit(solution)/shard_map/psum | solution.py:80
  10.2 3.6 %copy-start.2 = (s32[512]{0:T(512)S(1)}, s32[512]{0:T(512)}, u32[]{:S(2)}) copy-start(s32[512]{0:T(512)} %param.10) | copy-start | bytes 6148
  16.2 2.2 copy-start.4
  17.9 79.9 %all-gather.3.cloned.1.call-start = ((), (), s32[]{:S(2)}) async-start(), calls=%async_computation.6 | async-start | bytes 10813440 | tf_op jit(solution)/shard_map/all_gather | solution.py:87
  19.9 84.4 %all-to-all-start = ((s32[32,4,1]{1,2,0:T(1,128)}), s32[32,4,1]{1,2,0:T(1,128)S(1)}, u32[]{:S(2)}, u32[]{:S(2)}) async-start(s32[32,4,1]{1,2,0:T(1,128)} %bitcast), calls=%async_computation | async-start | bytes 32768 | tf_op jit(solution)/shard_map/all_to_all | solution.py:102
  97.8 18.0 %copy-start.3 = (bf16[1024]{0:T(1024)(128)(2,1)S(1)}, bf16[1024]{0:T(1024)(128)(2,1)}, u32[]{:S(2)}) copy-start(bf16[1024]{0:T(1024)(128)(2,1)} %param.17) | copy-start | bytes 6148
  104.3 20.9 %all-to-all-start.1 = ((bf16[32,4,1024]{2,1,0:T(4,128)(2,1)}), bf16[32,4,1024]{2,1,0:T(4,128)(2,1)S(1)}, u32[]{:S(2)}, u32[]{:S(2)}) async-start(bf16[32,4,1024]{2,1,0:T(4,128)(2,1)} %all_to_all.39), calls=%async_computation.1 | async-start | bytes 524288 | tf_op jit(solution)/shard_map/all_to_all | solution.py:101
  115.7 109.9 %all-gather.5.cloned.1.call-start = ((), (), s32[]{:S(2)}) async-start(), calls=%async_computation.7 | async-start | bytes 8650752 | tf_op jit(solution)/shard_map/all_gather | solution.py:121
  173.2 25.0 %all-to-all-start.3 = ((bf16[128,32,160]{0,2,1:T(8,128)(2,1)}), bf16[128,32,160]{0,2,1:T(8,128)(2,1)}, u32[]{:S(2)}, u32[]{:S(2)}) async-start(bf16[128,32,160]{0,2,1:T(8,128)(2,1)} %copy.39), calls=%async_computation.3 | async-start | bytes 2621440 | tf_op jit(solution)/shard_map/all_to_all | solution.py:83
Sparse Core Ops, SparseCore 0:
  18.0 77.2 all-reduce.1
Sparse Core Ops, SparseCore 1:
  20.9 66.7 all-gather.2
  165.3 60.3 all-gather.4
where the time goes:
time: 240 us; the launch traced here: 239 us
  waiting for transfers between devices  110 us (46%)
  matrix products  32.1 us (13%)
  blocking collectives  28.8 us (12%)
  starting transfers between devices  24.6 us (10%)
  local copies, waits for them, and re-layouts  21.8 us (9%)
  between operations  15.8 us (7%)
  other arithmetic  6.13 us (3%)
    psum x1, waiting for transfers between devices, shards(): lax.psum(partial_out.astype(jnp.bfloat16), 'tp').astype(jnp.float32)  66.8 us
    all_gather x1, waiting for transfers between devices, shards(): lax.all_gather(d_merged, 'ctx', axis=0, tiled=True)  27.4 us
    all_to_all x1, blocking collectives, shards(): lax.all_to_all(back_rows, 'ctx', split_axis=0, concat_axis=0, tiled=True)  17.6 us
    all_to_all x1, waiting for transfers between devices, shards(): lax.all_to_all(merged_in, 'ctx', split_axis=1, concat_axis=0, tiled=True)  15.3 us
    all_to_all x1, starting transfers between devices, shards(): lax.all_to_all(outgoing, 'ctx', split_axis=0, concat_axis=0, tiled=True)  11.4 us
    dot_general x3, matrix products, contract_rows(): lax.dot_general(left, right, (((0,), (0,)), ((), ())), preferred_element_...  11.4 us
    all_to_all x1, blocking collectives, sent_to_all(): return lax.all_to_all(copies, axis, split_axis=0, concat_axis=0, tiled=True)  11.2 us
    unnamed x13, local copies, waits for them, and re-layouts  10.5 us
  transfers between devices with their start and end apart: 6, of which 3 were waited for; matrix products, arithmetic and copies ran while one was open for 12% of the time, Pallas kernels for 0%

commit v1 on v0

--- a/solution.py
+++ b/solution.py
@@ -5,6 +5,11 @@
 
 D = 8192
 HEAD_DIM = 80
+
+
+def meet_domain(vec, axis_key, dimension_no):
+    formed = lax.all_to_all(jnp.stack(lax.axis_size(axis_key) * [vec]), axis_key, 0, 0)
+    return jnp.concatenate(formed, axis=dimension_no)
 
 
 def sent_to_all(shard, axis):
@@ -118,7 +123,7 @@
     returned = lax.all_to_all(back_rows, "ctx", split_axis=0, concat_axis=0, tiled=True)
     d_merged = contract_rows(select_mat, returned).astype(jnp.bfloat16)
     chosen = columns
-    merger_grad = contract_rows(chosen, lax.all_gather(d_merged, "ctx", axis=0, tiled=True))
+    merger_grad = contract_rows(chosen, meet_domain(d_merged, "ctx", 0))
     return (normed, merger_grad)
 
 

time: 240 us -> 339 us (1.41)
  the two profiles are of different devices: /device:TPU:1 before, /device:TPU:12 now
where the time goes in v1:
time: 339 us; the launch traced here: 338 us
  waiting for transfers between devices  206 us (61%)
  starting transfers between devices  37.8 us (11%)
  matrix products  30.3 us (9%)
  local copies, waits for them, and re-layouts  28.1 us (8%)
  between operations  15.8 us (5%)
  blocking collectives  12.7 us (4%)
  other arithmetic  7.41 us (2%)
    all_to_all x1, waiting for transfers between devices, meet_domain(): lax.all_to_all(jnp.stack(lax.axis_size(axis_key) * [vec]), axis_key, 0, 0)  118 us
    psum x1, waiting for transfers between devices, shards(): lax.psum(partial_out.astype(jnp.bfloat16), 'tp').astype(jnp.float32)  70.8 us
    all_to_all x1, waiting for transfers between devices, shards(): lax.all_to_all(merged_in, 'ctx', split_axis=1, concat_axis=0, tiled=True)  16.2 us
    all_to_all x1, blocking collectives, sent_to_all(): return lax.all_to_all(copies, axis, split_axis=0, concat_axis=0, tiled=True)  12.7 us
    unnamed x13, local copies, waits for them, and re-layouts  11.9 us
    dot_general x3, matrix products, contract_rows(): lax.dot_general(left, right, (((0,), (0,)), ((), ())), preferred_element_...  9.68 us
    all_to_all x1, starting transfers between devices, meet_domain(): lax.all_to_all(jnp.stack(lax.axis_size(axis_key) * [vec]), axis_key, 0, 0)  8.08 us
    all_to_all x2, local copies, waits for them, and re-layouts, shards(): lax.all_to_all(merged_in, 'ctx', split_axis=1, concat_axis=0, tiled=True)  7.98 us
  transfers between devices with their start and end apart: 7, of which 3 were waited for; matrix products, arithmetic and copies ran while one was open for 9% of the time, Pallas kernels for 0%

profile of v1, /device:TPU:12, one launch (start us, length us, event | category | flops | bytes accessed | tf_op | source)
XLA Modules:
  0.0 337.7 jit_solution(16323766392405445043)
XLA Ops:
  8.1 2.1 convolution_convert_fusion.7
  10.2 2.0 convolution_convert_fusion.5
  16.3 1.6 convolution_convert_fusion
  19.9 7.5 %all-to-all-start = ((s32[32,4,1]{1,2,0:T(1,128)}), s32[32,4,1]{1,2,0:T(1,128)S(1)}, u32[]{:S(2)}, u32[]{:S(2)}) async-start(s32[32,4,1]{1,2,0:T(1,128)} %bitcast), calls=%async_computation | async-start | bytes 32768 | tf_op jit(solution)/shard_map/all_to_all | solution.py:107
  27.4 70.8 %all-reduce.2.cloned.1.call-done = bf16[512,1280]{1,0:T(8,128)(2,1)} async-done(((bf16[512,1280]{1,0:T(8,128)(2,1)}), bf16[512,1280]{1,0:T(8,128)(2,1)}) %all-reduce.2.cloned.1.call-update) | async-done | bytes 1310736 | tf_op jit(solution)/shard_map/psum | solution.py:85
  98.2 1.6 add_convert_fusion
  100.7 5.7 %convolution_convert_fusion.2 = bf16[128,1024]{1,0:T(8,128)(2,1)S(1)} fusion(bf16[128,5120]{1,0:T(8,128)(2,1)S(1)} %reshape.121, bf16[5120,1024]{1,0:T(8,128)(2,1)} %all-gather.2.cloned.1.call-done, s32[128]{0:T(128)S(1)} %compare_select_fusion), kind=kOutput, calls=%fused_computation.19 | convolution fusion | flops 1376010240 | bytes 12059136 | tf_op jit(solution)/shard_map/dot_general | solution.py:101
  107.2 7.4 %all-to-all-start.1 = ((bf16[32,4,1024]{2,1,0:T(4,128)(2,1)}), bf16[32,4,1024]{2,1,0:T(4,128)(2,1)S(1)}, u32[]{:S(2)}, u32[]{:S(2)}) async-start(bf16[32,4,1024]{2,1,0:T(4,128)(2,1)} %all_to_all.40), calls=%async_computation.1 | async-start | bytes 524288 | tf_op jit(solution)/shard_map/all_to_all | solution.py:106
  114.6 3.9 %copy.36 = bf16[1024,1024]{0,1:T(8,128)(2,1)} copy(bf16[1024,1024]{1,0:T(8,128)(2,1)} %param.13) | data formatting | bytes 4194304 | tf_op args[4]
  118.6 4.0 %copy.35 = bf16[1024,1024]{0,1:T(8,128)(2,1)} copy(bf16[1024,1024]{1,0:T(8,128)(2,1)} %param.12) | data formatting | bytes 4194304 | tf_op args[3]
  124.1 5.5 %multiply_reduce_fusion.1 = (f32[1024]{0:T(1024)S(1)}, f32[1024]{0:T(1024)S(1)}, f32[1024,1024]{0,1:T(8,128)}) fusion(bf16[1024,1024]{0,1:T(8,128)(2,1)} %copy.36, f32[1024]{0:T(1024)S(1)} %convert_element_type.78, bf16[1024,1024]{0,1:T(8,128)(2,1)} %copy.35, bf16[128,1024]{1,0:T(8,128)(2,1)S(1)} %all_to_all.42, s32[128]{0:T(128)S(1)} %eq.74, ...), kind=kOutput, calls=%fused_computation.5 | convolution fusion | flops 276953088 | bytes 8664576 | tf_op jit(solution)/shard_map/dot_general | solution.py:111
  129.7 12.7 %all_to_all.57 = f32[8,1,2048]{2,1,0:T(1,128)S(1)} all-to-all(f32[8,1,2048]{2,1,0:T(1,128)S(1)} %broadcast_in_dim.73), channel_id=1, replica_groups=mesh['ctx'=32,'tp'=8] {'tp'}, dimensions={0} | all-to-all | bytes 131072 | tf_op jit(solution)/shard_map/all_to_all | solution.py:17
  142.4 4.3 %fusion.8 = bf16[128,1024]{1,0:T(8,128)(2,1)S(1)} fusion(f32[1024,1024]{0,1:T(8,128)} %get-tuple-element.37, bf16[1024,1024]{0,1:T(8,128)(2,1)} %copy.36, f32[1024]{0:T(1024)S(1)} %get-tuple-element.34, f32[1024]{0:T(1024)S(1)} %get-tuple-element.32, f32[1024]{0:T(1024)S(1)} %get-tuple-element.33, f32[1024]{0:T(1024)S(1)} %convert_element_type.78, ...), kind=kOutput, calls=%fused_computation.17 | convolution fusion | flops 277217280 | bytes 6570496 | tf_op jit(solution)/shard_map/dot_general | solution.py:63
  147.5 7.4 %all-to-all-start.4 = ((bf16[32,4,1024]{2,1,0:T(4,128)(2,1)}), bf16[32,4,1024]{2,1,0:T(4,128)(2,1)S(1)}, u32[]{:S(2)}, u32[]{:S(2)}) async-start(bf16[32,4,1024]{2,1,0:T(4,128)(2,1)} %all_to_all.47), calls=%async_computation.4 | async-start | bytes 524288 | tf_op jit(solution)/shard_map/all_to_all | solution.py:123
  154.9 3.6 %all_to_all.44 = bf16[128,32,160]{2,1,0:T(8,128)(2,1)} reshape(bf16[512,1280]{1,0:T(8,128)(2,1)S(1)} %add_convert_fusion) | data formatting | bytes 2621440 | tf_op jit(solution)/shard_map/all_to_all | solution.py:88
  158.5 4.3 %copy.38 = bf16[128,32,160]{0,2,1:T(8,128)(2,1)} copy(bf16[128,32,160]{2,1,0:T(8,128)(2,1)} %all_to_all.44) | data formatting | bytes 2621440 | tf_op jit(solution)/shard_map/all_to_all | solution.py:88
  162.8 7.4 %all-to-all-start.3 = ((bf16[128,32,160]{0,2,1:T(8,128)(2,1)}), bf16[128,32,160]{0,2,1:T(8,128)(2,1)S(1)}, u32[]{:S(2)}, u32[]{:S(2)}) async-start(bf16[128,32,160]{0,2,1:T(8,128)(2,1)} %copy.38), calls=%async_computation.3 | async-start | bytes 2621440 | tf_op jit(solution)/shard_map/all_to_all | solution.py:88
  170.6 16.2 %all-to-all-done.3 = bf16[128,32,160]{0,2,1:T(8,128)(2,1)S(1)} async-done(((bf16[128,32,160]{0,2,1:T(8,128)(2,1)}), bf16[128,32,160]{0,2,1:T(8,128)(2,1)S(1)}, u32[]{:S(2)}, u32[]{:S(2)}) %all-to-all-start.3) | async-done | bytes 1310752 | tf_op jit(solution)/shard_map/all_to_all | solution.py:88
  186.8 4.3 %stack.2 = bf16[32,128,1024]{2,1,0:T(8,128)(2,1)} broadcast(bf16[128,1024]{1,0:T(8,128)(2,1)S(1)} %convolution_convert_fusion.1), dimensions={1,2} | broadcast | bytes 8650752 | tf_op jit(solution)/shard_map/stack | solution.py:11
  191.1 8.1 %all-to-all-start.5 = ((bf16[32,128,1024]{2,1,0:T(8,128)(2,1)}), bf16[32,128,1024]{2,1,0:T(8,128)(2,1)}, u32[]{:S(2)}, u32[]{:S(2)}) async-start(bf16[32,128,1024]{2,1,0:T(8,128)(2,1)} %stack.2), calls=%async_computation.5 | async-start | bytes 16777216 | tf_op jit(solution)/shard_map/all_to_all | solution.py:11
  199.2 3.9 %multiply_convert_fusion = bf16[1024,1024]{0,1:T(8,128)(2,1)} fusion(f32[1024,1024]{0,1:T(8,128)} %get-tuple-element.37, f32[1024]{0:T(1024)S(1)} %get-tuple-element.33, f32[1024]{0:T(1024)S(1)} %convert_element_type.78), kind=kLoop, calls=%fused_computation.2 | loop fusion | flops 3145728 | bytes 6299648 | tf_op jit(solution)/shard_map/convert_element_type | solution.py:120
  203.1 3.9 %copy.39 = bf16[1024,1024]{1,0:T(8,128)(2,1)} copy(bf16[1024,1024]{0,1:T(8,128)(2,1)} %multiply_convert_fusion) | data formatting | bytes 4194304
  207.0 118.1 %all-to-all-done.5 = bf16[32,128,1024]{2,1,0:T(8,128)(2,1)} async-done(((bf16[32,128,1024]{2,1,0:T(8,128)(2,1)}), bf16[32,128,1024]{2,1,0:T(8,128)(2,1)}, u32[]{:S(2)}, u32[]{:S(2)}) %all-to-all-start.5) | async-done | bytes 8388640 | tf_op jit(solution)/shard_map/all_to_all | solution.py:11
  325.1 5.2 %fusion.5 = f32[160,1024]{1,0:T(8,128)} fusion(bf16[32,128,1024]{2,1,0:T(8,128)(2,1)} %all-to-all-done.5, bf16[128,32,160]{0,2,1:T(8,128)(2,1)S(1)} %all-to-all-done.3), kind=kOutput, calls=%fused_computation.16 | convolution fusion | flops 1342177280 | bytes 10354688 | tf_op jit(solution)/shard_map/dot_general | solution.py:63
  (47 shorter events, 10.6 us)
Async XLA Ops:
  8.0 8.3 %copy-start = (bf16[160,1280]{1,0:T(8,128)(2,1)S(1)}, bf16[160,1280]{1,0:T(8,128)(2,1)}, u32[]{:S(2)}) copy-start(bf16[160,1280]{1,0:T(8,128)(2,1)} %param.15) | copy-start | bytes 1228804
  8.0 4.1 %copy-start.1 = (bf16[512,1280]{1,0:T(8,128)(2,1)S(1)}, bf16[512,1280]{1,0:T(8,128)(2,1)}, u32[]{:S(2)}) copy-start(bf16[512,1280]{1,0:T(8,128)(2,1)} %param.9) | copy-start | bytes 3932164
  8.0 90.2 %all-reduce.2.cloned.1.call-start = ((), (), s32[]{:S(2)}) async-start(), calls=%async_computation.6 | async-start | bytes 2621440 | tf_op jit(solution)/shard_map/psum | solution.py:85
  10.2 3.6 %copy-start.2 = (s32[512]{0:T(512)S(1)}, s32[512]{0:T(512)}, u32[]{:S(2)}) copy-start(s32[512]{0:T(512)} %param.10) | copy-start | bytes 6148
  16.2 2.2 copy-start.4
  17.9 82.8 %all-gather.2.cloned.1.call-start = ((), (), s32[]{:S(2)}) async-start(), calls=%async_computation.7 | async-start | bytes 10813440 | tf_op jit(solution)/shard_map/all_gather | solution.py:92
  19.9 87.3 %all-to-all-start = ((s32[32,4,1]{1,2,0:T(1,128)}), s32[32,4,1]{1,2,0:T(1,128)S(1)}, u32[]{:S(2)}, u32[]{:S(2)}) async-start(s32[32,4,1]{1,2,0:T(1,128)} %bitcast), calls=%async_computation | async-start | bytes 32768 | tf_op jit(solution)/shard_map/all_to_all | solution.py:107
  100.7 13.9 %copy-start.3 = (bf16[1024]{0:T(1024)(128)(2,1)S(1)}, bf16[1024]{0:T(1024)(128)(2,1)}, u32[]{:S(2)}) copy-start(bf16[1024]{0:T(1024)(128)(2,1)} %param.17) | copy-start | bytes 6148
  107.2 16.8 %all-to-all-start.1 = ((bf16[32,4,1024]{2,1,0:T(4,128)(2,1)}), bf16[32,4,1024]{2,1,0:T(4,128)(2,1)S(1)}, u32[]{:S(2)}, u32[]{:S(2)}) async-start(bf16[32,4,1024]{2,1,0:T(4,128)(2,1)} %all_to_all.40), calls=%async_computation.1 | async-start | bytes 524288 | tf_op jit(solution)/shard_map/all_to_all | solution.py:106
  147.5 15.4 %all-to-all-start.4 = ((bf16[32,4,1024]{2,1,0:T(4,128)(2,1)}), bf16[32,4,1024]{2,1,0:T(4,128)(2,1)S(1)}, u32[]{:S(2)}, u32[]{:S(2)}) async-start(bf16[32,4,1024]{2,1,0:T(4,128)(2,1)} %all_to_all.47), calls=%async_computation.4 | async-start | bytes 524288 | tf_op jit(solution)/shard_map/all_to_all | solution.py:123
  162.8 24.0 %all-to-all-start.3 = ((bf16[128,32,160]{0,2,1:T(8,128)(2,1)}), bf16[128,32,160]{0,2,1:T(8,128)(2,1)S(1)}, u32[]{:S(2)}, u32[]{:S(2)}) async-start(bf16[128,32,160]{0,2,1:T(8,128)(2,1)} %copy.38), calls=%async_computation.3 | async-start | bytes 2621440 | tf_op jit(solution)/shard_map/all_to_all | solution.py:88
  191.1 134.0 %all-to-all-start.5 = ((bf16[32,128,1024]{2,1,0:T(8,128)(2,1)}), bf16[32,128,1024]{2,1,0:T(8,128)(2,1)}, u32[]{:S(2)}, u32[]{:S(2)}) async-start(bf16[32,128,1024]{2,1,0:T(8,128)(2,1)} %stack.2), calls=%async_computation.5 | async-start | bytes 16777216 | tf_op jit(solution)/shard_map/all_to_all | solution.py:11
Sparse Core Ops, SparseCore 0:
  18.0 80.1 all-reduce.1
Sparse Core Ops, SparseCore 1:
  20.9 64.0 all-gather.1
